TPU v7x, 16 devices: a 4x2x1 block of a 4x4x8 slice. The times are simulated.
16 devices in a mesh: dp: 4 (over y, z, core), tp: 4 (over x).
Axes of the slice: x: 4, y: 2, z: 1, core: 2. Of those that a mesh axis runs over, the one named last changes fastest.
The devices are a block of a 4x4x8 slice.
Arguments:
- x: bfloat16 [512, 7168], P('dp'), parts along dimension 0
- w_gate: bfloat16 [7168, 20480], P(None, 'tp')
- w_up: bfloat16 [7168, 20480], P(None, 'tp')
- w_down: bfloat16 [20480, 7168], P('tp')
Outputs:
- output: bfloat16 [512, 7168], P('dp'), parts along dimension 0
There are 4 independent parts. A program takes and returns all parts, laid end to end along the dimension named above; an argument that names none is the same for every part.
All inputs are finite; a program needn't handle non-finite values.
Results may differ from a plain program's by a relative error of at most 0.016.
Values are sent between devices in bfloat16 or wider.
A program may use at most 768 MiB of HBM per device.

v0:
```python
import jax
import jax.numpy as jnp
from jax import lax
from jax.sharding import PartitionSpec as P


def solution(mesh):
    def step(x, w_gate, w_up, w_down):
        gate = jnp.dot(x, w_gate, preferred_element_type=jnp.float32)
        up = jnp.dot(x, w_up, preferred_element_type=jnp.float32)
        hidden = (jax.nn.silu(gate) * up).astype(jnp.bfloat16)
        term = jnp.dot(hidden, w_down, preferred_element_type=jnp.float32).astype(jnp.bfloat16)
        return lax.psum(term, "tp")

    return jax.shard_map(
        step,
        mesh=mesh,
        in_specs=(P("dp", None), P(None, "tp"), P(None, "tp"), P("tp", None)),
        out_specs=P("dp", None),
        check_vma=False,
    )
```

profile of v0, /device:TPU:112, one launch (start us, length us, event | category | flops | bytes accessed | tf_op | source)
XLA Modules:
  0.0 145.5 jit_solution(6335706506732981648)
XLA Ops:
  6.5 0.0 copy-start
  6.6 0.0 all-reduce.2.cloned.1.call-start
  6.6 1.5 %copy-done = bf16[128,7168]{1,0:T(8,128)(2,1)S(1)} copy-done((bf16[128,7168]{1,0:T(8,128)(2,1)S(1)}, bf16[128,7168]{1,0:T(8,128)(2,1)}, u32[]{:S(2)}) %copy-start) | copy-done | bytes 1835032
  8.1 26.3 %fusion.8 = f32[128,5120]{1,0:T(8,128)} fusion(bf16[128,7168]{1,0:T(8,128)(2,1)S(1)} %copy-done, bf16[7168,5120]{1,0:T(8,128)(2,1)} %param.5), kind=kOutput, calls=%fused_computation.10 | convolution fusion | flops 9395240960 | bytes 77856768 | tf_op jit(solution)/shard_map/dot_general | solution.py:9
  34.3 26.2 %fusion.clone.4 = bf16[128,5120]{1,0:T(8,128)(2,1)S(1)} fusion(bf16[128,7168]{1,0:T(8,128)(2,1)S(1)} %copy-done, bf16[7168,5120]{1,0:T(8,128)(2,1)} %param.6, f32[128,5120]{1,0:T(8,128)} %fusion.8), kind=kOutput, calls=%fused_computation.2.clone.clone.clone.1 | convolution fusion | flops 9399173120 | bytes 79167488 | tf_op jit(solution)/shard_map/dot_general | solution.py:10
  60.5 26.2 %convolution_convert_fusion = bf16[128,7168]{1,0:T(8,128)(2,1)} fusion(bf16[5120,7168]{1,0:T(8,128)(2,1)} %param.7, bf16[128,5120]{1,0:T(8,128)(2,1)S(1)} %fusion.clone.4), kind=kOutput, calls=%fused_computation | convolution fusion | flops 9396158464 | bytes 76546048 | tf_op jit(solution)/shard_map/dot_general | solution.py:12
  86.7 0.1 all-reduce.2.cloned.1.call-update
  86.7 49.1 %all-reduce.2.cloned.1.call-done = bf16[128,7168]{1,0:T(8,128)(2,1)} async-done(((bf16[128,7168]{1,0:T(8,128)(2,1)}), bf16[128,7168]{1,0:T(8,128)(2,1)}) %all-reduce.2.cloned.1.call-update) | async-done | bytes 1835024 | tf_op jit(solution)/shard_map/psum | solution.py:13
  135.8 2.8 %copy.6 = bf16[128,7168]{1,0:T(8,128)(2,1)} copy(bf16[128,7168]{1,0:T(8,128)(2,1)} %all-reduce.2.cloned.1.call-done) | data formatting | bytes 3670016
Async XLA Ops:
  6.5 1.5 %copy-start = (bf16[128,7168]{1,0:T(8,128)(2,1)S(1)}, bf16[128,7168]{1,0:T(8,128)(2,1)}, u32[]{:S(2)}) copy-start(bf16[128,7168]{1,0:T(8,128)(2,1)} %param.4) | copy-start | bytes 5505028
  6.6 129.2 %all-reduce.2.cloned.1.call-start = ((), (), s32[]{:S(2)}) async-start(), calls=%async_computation | async-start | bytes 3670016 | tf_op jit(solution)/shard_map/psum | solution.py:13
Sparse Core Ops, SparseCore 0:
  86.9 48.8 all-reduce.1
where the time goes:
time: 146 us; the launch traced here: 145 us
  matrix products  78.6 us (54%)
  waiting for transfers between devices  49.1 us (34%)
  between operations  13.4 us (9%)
  local copies, waits for them, and re-layouts  4.34 us (3%)
    psum x1, waiting for transfers between devices, step(): return lax.psum(term, 'tp')  49.1 us
    dot_general x1, matrix products, step(): gate = jnp.dot(x, w_gate, preferred_element_type=jnp.float32)  26.3 us
    dot_general x1, matrix products, step(): up = jnp.dot(x, w_up, preferred_element_type=jnp.float32)  26.2 us
    dot_general x1, matrix products, step(): jnp.dot(hidden, w_down, preferred_element_type=jnp.float32)  26.2 us
    unnamed x3, local copies, waits for them, and re-layouts  4.34 us
  transfers between devices with their start and end apart: 1, of which 1 were waited for; matrix products, arithmetic and copies ran while one was open for 0% of the time, Pallas kernels for 0%

commit v1 on v0

v1 whole, which is shorter than its diff:
```python
import functools

import jax
import jax.numpy as jnp
from jax import lax
from jax.experimental import pallas as pl
from jax.experimental.pallas import tpu as pltpu
from jax.sharding import PartitionSpec as P

MESH = pl.DeviceIdType.MESH
HB = 256
NS = 4
CB = 512
ND = 6
LAG_A = 5
LAG_F = 14
LAG_G = 20


def kernel(
    x_ref, wg_ref, wu_ref, wd_ref, y_ref,
    xbuf, wg, wu, wd, hid, acc, d2d_out, d2d_in, s1_out, s1_in, s2_out, s2_in,
    x_sem, xs_sem, xr_sem, g_sem, u_sem, d_sem, c_send, c_recv,
    s1_send, s1_recv, s2b_send, s2b_recv, s2a_send, s2a_recv, s3_send, s3_recv, s4_send, s4_recv,
):
    rows, d = x_ref.shape
    ff = wg_ref.shape[1] // 2
    n = 4
    nb = ff // HB
    np_ = d // CB
    q = rows // n
    h = q // 2
    dp, tp = lax.axis_index("dp"), lax.axis_index("tp")
    core = lax.rem(dp, 2)
    peer = {"dp": dp + 1 - 2 * core, "tp": tp}
    right = {"dp": dp, "tp": lax.rem(tp + 1, n)}
    left = {"dp": dp, "tp": lax.rem(tp + n - 1, n)}
    me_rows = pl.multiple_of(tp * q, q)
    right_rows = pl.multiple_of(lax.rem(tp + 1, n) * q, q)
    far_rows = pl.multiple_of(lax.rem(tp + 2, n) * q, q)
    left_rows = pl.multiple_of(lax.rem(tp + 3, n) * q, q)
    base = core * ff

    def gate_copy(j):
        cols = pl.ds(pl.multiple_of(base + j * HB, HB), HB)
        s = lax.rem(j, NS)
        return pltpu.make_async_copy(wg_ref.at[:, cols], wg.at[s], g_sem.at[s])

    def up_copy(j):
        cols = pl.ds(pl.multiple_of(base + j * HB, HB), HB)
        s = lax.rem(j, NS)
        return pltpu.make_async_copy(wu_ref.at[:, cols], wu.at[s], u_sem.at[s])

    def down_copy(p):
        s = lax.rem(p, ND)
        return pltpu.make_async_copy(
            wd_ref.at[pl.ds(pl.multiple_of(base, HB), ff), pl.ds(pl.multiple_of(p * CB, CB), CB)],
            wd.at[s], d_sem.at[s])

    own_x = pltpu.make_async_copy(x_ref, xbuf.at[pl.ds(0, rows)], x_sem)
    own_x.start()
    gate_copy(0).start()
    up_copy(0).start()

    barrier = pltpu.get_barrier_semaphore()
    for other in (peer, left, right):
        pl.semaphore_signal(barrier, inc=1, device_id=other, device_id_type=MESH)
    for j in range(1, NS):
        gate_copy(j).start()
        up_copy(j).start()
    pl.semaphore_wait(barrier, 3)

    peer_x = pltpu.make_async_remote_copy(
        src_ref=x_ref, dst_ref=xbuf.at[pl.ds(rows, rows)], send_sem=xs_sem, recv_sem=xr_sem,
        device_id=peer, device_id_type=MESH)
    peer_x.start()

    def gate_up(j, r0, nr):
        s = lax.rem(j, NS)
        xs = xbuf[pl.ds(r0, nr), :]
        g = jnp.dot(xs, wg[s], preferred_element_type=jnp.float32)
        u = jnp.dot(xs, wu[s], preferred_element_type=jnp.float32)
        hid[pl.ds(r0, nr), pl.ds(pl.multiple_of(j * HB, HB), HB)] = (jax.nn.silu(g) * u).astype(hid.dtype)

    own_x.wait()
    gate_copy(0).wait()
    up_copy(0).wait()
    gate_up(0, 0, rows)
    peer_x.wait_recv()
    gate_up(0, rows, rows)
    gate_copy(NS).start()
    up_copy(NS).start()

    for p in range(ND):
        down_copy(p).start()

    @pl.loop(1, nb)
    def _(j):
        gate_copy(j).wait()
        up_copy(j).wait()
        gate_up(j, 0, 2 * rows)

        @pl.when(j + NS < nb)
        def _():
            gate_copy(j + NS).start()
            up_copy(j + NS).start()

    def cols_of(p):
        return pl.ds(pl.multiple_of(p * CB, CB), CB)

    def rcopy(src, dst, send, recv, to):
        return pltpu.make_async_remote_copy(
            src_ref=src, dst_ref=dst, send_sem=send, recv_sem=recv, device_id=to, device_id_type=MESH)

    def pair_copy(p):
        c = cols_of(p)
        return rcopy(d2d_out.at[:, c], d2d_in.at[:, c], c_send.at[p], c_recv.at[p], peer)

    def first_hop(p):
        c = cols_of(p)
        return [rcopy(s1_out.at[i, :, c], s1_in.at[i, :, c], s1_send.at[i, p], s1_recv.at[i, p], to)
                for i, to in enumerate((right, left))]

    def second_hop(p, summed):
        c = cols_of(p)
        out = []
        for i, to in enumerate((right, left)):
            r = pl.ds(h * ((i + (0 if summed else 1)) % 2), h)
            send, recv = (s2a_send, s2a_recv) if summed else (s2b_send, s2b_recv)
            out.append(rcopy(s2_out.at[i, r, c], s2_in.at[i, r, c], send.at[i, p], recv.at[i, p], to))
        return out

    def finished(p, send_side=True):
        c = cols_of(p)
        r = pl.ds(me_rows, q)
        return [rcopy(y_ref.at[r, c], y_ref.at[r, c], s3_send.at[i, p], s3_recv.at[i, p], to)
                for i, to in enumerate((right, left))]

    def forward(p):
        c = cols_of(p)
        ra = pl.ds(pl.multiple_of(left_rows, h), h)
        rb = pl.ds(pl.multiple_of(right_rows + h, h), h)
        return [rcopy(y_ref.at[r, c], y_ref.at[r, c], s4_send.at[i, p], s4_recv.at[i, p], to)
                for i, (r, to) in enumerate(((ra, right), (rb, left)))]

    @pl.loop(0, np_ + LAG_G)
    def _(it):
        @pl.when(it < np_)
        def _():
            p = it
            c = cols_of(p)
            down_copy(p).wait()
            t = jnp.dot(hid[...], wd[lax.rem(p, ND)], preferred_element_type=jnp.float32)
            d2d_out[:, c] = t[rows:].astype(d2d_out.dtype)
            acc[:, c] = t[:rows]
            pair_copy(p).start()

            @pl.when(p + ND < np_)
            def _():
                down_copy(p + ND).start()

        @pl.when((it >= 1) & (it < np_ + 1))
        def _():
            p = it - 1
            c = cols_of(p)
            pair_copy(p).wait_recv()
            acc[:, c] += d2d_in[:, c].astype(jnp.float32)
            s1_out[0, :, c] = acc[pl.ds(far_rows, h), c].astype(s1_out.dtype)
            s1_out[1, :, c] = acc[pl.ds(pl.multiple_of(far_rows + h, h), h), c].astype(s1_out.dtype)
            s2_out[0, pl.ds(h, h), c] = acc[pl.ds(pl.multiple_of(right_rows + h, h), h), c].astype(s2_out.dtype)
            s2_out[1, pl.ds(0, h), c] = acc[pl.ds(left_rows, h), c].astype(s2_out.dtype)
            for cp in first_hop(p) + second_hop(p, False):
                cp.start()

        @pl.when((it >= LAG_A) & (it < np_ + LAG_A))
        def _():
            p = it - LAG_A
            c = cols_of(p)
            for cp in first_hop(p):
                cp.wait_recv()
            s2_out[0, pl.ds(0, h), c] = (
                acc[pl.ds(right_rows, h), c] + s1_in[0, :, c].astype(jnp.float32)).astype(s2_out.dtype)
            s2_out[1, pl.ds(h, h), c] = (
                acc[pl.ds(pl.multiple_of(left_rows + h, h), h), c] + s1_in[1, :, c].astype(jnp.float32)
            ).astype(s2_out.dtype)
            for cp in second_hop(p, True):
                cp.start()

        @pl.when((it >= LAG_F) & (it < np_ + LAG_F))
        def _():
            p = it - LAG_F
            c = cols_of(p)
            for cp in second_hop(p, False) + second_hop(p, True):
                cp.wait_recv()
            y_ref[pl.ds(me_rows, q), c] = (
                acc[pl.ds(me_rows, q), c] + s2_in[0, :, c].astype(jnp.float32)
                + s2_in[1, :, c].astype(jnp.float32)).astype(y_ref.dtype)
            for cp in finished(p):
                cp.start()

        @pl.when(it >= LAG_G)
        def _():
            p = it - LAG_G
            for cp in finished(p):
                cp.wait_recv()
            for cp in forward(p):
                cp.start()

    peer_x.wait_send()

    @pl.loop(0, np_)
    def _(p):
        pair_copy(p).wait_send()
        for cp in first_hop(p) + second_hop(p, False) + second_hop(p, True) + finished(p):
            cp.wait_send()
        for cp in forward(p):
            cp.wait()


def solution(mesh):
    def step(x, w_gate, w_up, w_down):
        rows, d = x.shape
        ff = w_gate.shape[1] // 2
        q = rows // mesh.shape["tp"]
        np_ = d // CB
        bf, f32 = jnp.bfloat16, jnp.float32
        dma = pltpu.SemaphoreType.DMA
        hbm = pl.BlockSpec(memory_space=pl.ANY)
        return pl.pallas_call(
            kernel,
            out_shape=jax.ShapeDtypeStruct((rows, d), x.dtype),
            in_specs=[hbm] * 4,
            out_specs=pl.BlockSpec(memory_space=pltpu.VMEM),
            scratch_shapes=[
                pltpu.VMEM((2 * rows, d), bf),
                pltpu.VMEM((NS, d, HB), bf),
                pltpu.VMEM((NS, d, HB), bf),
                pltpu.VMEM((ND, ff, CB), bf),
                pltpu.VMEM((2 * rows, ff), bf),
                pltpu.VMEM((rows, d), f32),
                pltpu.VMEM((rows, d), bf),
                pltpu.VMEM((rows, d), bf),
                pltpu.VMEM((2, q // 2, d), bf),
                pltpu.VMEM((2, q // 2, d), bf),
                pltpu.VMEM((2, q, d), bf),
                pltpu.VMEM((2, q, d), bf),
                dma, dma, dma, dma((NS,)), dma((NS,)), dma((ND,)), dma((np_,)), dma((np_,)),
            ] + [dma((2, np_))] * 10,
            compiler_params=pltpu.CompilerParams(
                collective_id=0, has_side_effects=True, vmem_limit_bytes=67043328),
        )(x, w_gate, w_up, w_down)

    return jax.shard_map(
        step,
        mesh=mesh,
        in_specs=(P("dp", None), P(None, "tp"), P(None, "tp"), P("tp", None)),
        out_specs=P("dp", None),
        check_vma=False,
    )
```

time: 146 us -> 75.2 us (0.52)
  matrix products: 78.6 us -> 0 us
  Pallas kernels: 0 us -> 72.2 us
  waiting for transfers between devices: 49.1 us -> 0 us
  between operations: 13.4 us -> 0.01 us
  local copies, waits for them, and re-layouts: 4.34 us -> 2.85 us
    dot_general x3 -> x0, matrix products: 78.6 us -> none  [the longest x1 26.3 us: step(): gate = jnp.dot(x, w_gate, preferred_element_type=jnp.float32)]
    pallas_call x0 -> x1, Pallas kernels: none -> 72.2 us  [step(): pl.pallas_call(kernel, out_shape=jax.ShapeDtypeStruct((rows, d), x.dtype)...]
    psum x1 -> x0, waiting for transfers between devices: 49.1 us -> none  [step(): return lax.psum(term, 'tp')]
    unnamed x3 -> x1, local copies, waits for them, and re-layouts: 4.34 us -> 2.85 us
  transfers between devices with their start and end apart: 1 -> 0, of which waited for: 1 -> 0; matrix products, arithmetic and copies ran while one was open for 0% -> 0% of each run, Pallas kernels for 0% -> 0%
where the time goes in v1:
time: 75.2 us; the launch traced here: 75.1 us
  Pallas kernels  72.2 us (96%)
  local copies, waits for them, and re-layouts  2.85 us (4%)
    pallas_call x1, Pallas kernels, step(): pl.pallas_call(kernel, out_shape=jax.ShapeDtypeStruct((rows, d), x.dtype)...  72.2 us
    unnamed x1, local copies, waits for them, and re-layouts  2.85 us

profile of v1, /device:TPU:112, one launch (start us, length us, event | category | flops | bytes accessed | tf_op | source)
XLA Modules:
  0.0 75.1 jit_solution(16426068036820499131)
XLA Ops:
  0.0 72.2 %shard_map.46 = bf16[128,7168]{1,0:T(8,128)(2,1)} custom-call(bf16[128,7168]{1,0:T(8,128)(2,1)} %x_ref.1, bf16[7168,5120]{1,0:T(8,128)(2,1)} %wg_ref.1, bf16[7168,5120]{1,0:T(8,128)(2,1)} %wu_ref.1, bf16[5120,7168]{1,0:T(8,128)(2,1)} %wd_ref.1), custom_call_target="tpu_custom_call" | custom-call | tf_op jit(solution)/shard_map/pallas_call | solution.py:229
  72.2 2.8 %copy.6 = bf16[128,7168]{1,0:T(8,128)(2,1)} copy(bf16[128,7168]{1,0:T(8,128)(2,1)} %shard_map.46) | data formatting | bytes 3670016

commit v2 on v0

v2 whole, which is shorter than its diff:
```python
import jax
import jax.numpy as jnp
from jax import lax
from jax.experimental import pallas as pl
from jax.experimental.pallas import tpu as pltpu
from jax.sharding import PartitionSpec as P

MESH = pl.DeviceIdType.MESH
F32 = jnp.float32
HB = 256
NS = 4
OWN = 2
CB = 512
ND = 3
LB = 2
LF = 7
LG = 11


def kernel(
    x_ref, wg_ref, wu_ref, wd_ref, y_ref,
    xbuf, wg, wu, wd, hid, k_me, k_n, a_out, a_in, b_out, b_in, f_out,
    x_sem, xs_sem, xr_sem, g_sem, u_sem, d_sem, h_send, h_recv,
    a_send, a_recv, b_send, b_recv, f_send, f_recv, l_send, l_recv, g_send, g_recv,
):
    rows, d = x_ref.shape
    ff = wg_ref.shape[1] // 2
    dh = d // 2
    n = 4
    nb = ff // HB
    nc = dh // CB
    q = rows // n
    h = q // 2
    dp, tp = lax.axis_index("dp"), lax.axis_index("tp")
    core = lax.rem(dp, 2)
    other = 1 - core
    dp_peer = dp + 1 - 2 * core
    tp_r, tp_f, tp_l = [lax.rem(tp + i, n) for i in (1, 2, 3)]
    peer = {"dp": dp_peer, "tp": tp}
    side = [{"dp": dp, "tp": tp_r}, {"dp": dp, "tp": tp_l}]
    side_peer = [{"dp": dp_peer, "tp": tp_r}, {"dp": dp_peer, "tp": tp_l}]
    base = core * ff
    cbase = core * dh
    own_r = pl.multiple_of(core * rows, rows)
    peer_r = pl.multiple_of(other * rows, rows)

    def remote(src, dst, send, recv, to):
        return pltpu.make_async_remote_copy(
            src_ref=src, dst_ref=dst, send_sem=send, recv_sem=recv, device_id=to, device_id_type=MESH)

    def hcols(j):
        return pl.ds(pl.multiple_of(base + j * HB, HB), HB)

    def gate_copy(j):
        s = lax.rem(j, NS)
        return pltpu.make_async_copy(wg_ref.at[:, hcols(j)], wg.at[s], g_sem.at[s])

    def up_copy(j):
        s = lax.rem(j, NS)
        return pltpu.make_async_copy(wu_ref.at[:, hcols(j)], wu.at[s], u_sem.at[s])

    def down_copy(m):
        s = lax.rem(m, ND)
        src = wd_ref.at[:, pl.ds(pl.multiple_of(cbase + m * CB, CB), CB)]
        return pltpu.make_async_copy(src, wd.at[s], d_sem.at[s])

    def hid_copy(j):
        return remote(hid.at[:, hcols(j)], hid.at[:, hcols(j)], h_send.at[j], h_recv.at[j], peer)

    own_x = pltpu.make_async_copy(x_ref, xbuf.at[pl.ds(own_r, rows)], x_sem)
    own_x.start()
    gate_copy(0).start()
    up_copy(0).start()
    barrier = pltpu.get_barrier_semaphore()
    for to in [peer] + side + side_peer:
        pl.semaphore_signal(barrier, inc=1, device_id=to, device_id_type=MESH)
    for j in range(1, NS):
        gate_copy(j).start()
        up_copy(j).start()
    own_x.wait()
    pl.semaphore_wait(barrier, 5)
    peer_x = remote(xbuf.at[pl.ds(own_r, rows)], xbuf.at[pl.ds(own_r, rows)], xs_sem, xr_sem, peer)
    peer_x.start()

    def gate_up(j, r0, nr):
        s = lax.rem(j, NS)
        xs = xbuf[pl.ds(r0, nr), :]
        g = jnp.dot(xs, wg[s], preferred_element_type=F32)
        u = jnp.dot(xs, wu[s], preferred_element_type=F32)
        hid[pl.ds(r0, nr), hcols(j)] = (jax.nn.silu(g) * u).astype(hid.dtype)

    def refill(j):
        @pl.when(j + NS < nb)
        def _():
            gate_copy(j + NS).start()
            up_copy(j + NS).start()

        @pl.when(j + NS == nb)
        def _():
            for m in range(ND):
                down_copy(m).start()

    @pl.loop(0, OWN)
    def _(j):
        gate_copy(j).wait()
        up_copy(j).wait()
        gate_up(j, own_r, rows)

    peer_x.wait_recv()

    @pl.loop(0, OWN)
    def _(j):
        gate_up(j, peer_r, rows)
        refill(j)

    @pl.loop(OWN, nb)
    def _(j):
        gate_copy(j).wait()
        up_copy(j).wait()

        @pl.when(j == OWN)
        def _():
            for i in range(OWN - 1):
                hid_copy(i).start()

        hid_copy(j - 1).start()
        gate_up(j, 0, 2 * rows)
        refill(j)

    hid_copy(nb - 1).start()

    def chunk(m):
        return pl.ds(pl.multiple_of(m * CB, CB), CB)

    def ycols(c, half):
        return pl.ds(pl.multiple_of(half * dh + c * CB, CB), CB)

    def a_copies(m):
        c = chunk(m)
        return [remote(a_out.at[i, :, :, :, c], a_in.at[i, :, :, :, c], a_send.at[i, m], a_recv.at[i, m], side[i])
                for i in range(2)]

    def b_copies(m):
        c = chunk(m)
        return [remote(b_out.at[i, :, :, c], b_in.at[i, :, :, c], b_send.at[i, m], b_recv.at[i, m], side[i])
                for i in range(2)]

    me_rows = pl.ds(pl.multiple_of(tp * q, q), q)

    def f_copies(m):
        c = ycols(m, core)
        out = []
        for i in range(2):
            out.append(remote(y_ref.at[me_rows, c], y_ref.at[me_rows, c], f_send.at[i, 0, m],
                              f_recv.at[i, core, m], side[i]))
            out.append(remote(f_out.at[:, chunk(m)], y_ref.at[me_rows, c], f_send.at[i, 1, m],
                              f_recv.at[i, core, m], side_peer[i]))
        return out

    def f_waits(m):
        return [remote(y_ref.at[me_rows, ycols(m, e)], y_ref.at[me_rows, ycols(m, e)], f_send.at[i, 0, m],
                       f_recv.at[i, e, m], side[i]) for i in range(2) for e in range(2)]

    def l_copy(m):
        c = ycols(m, core)
        return remote(f_out.at[:, chunk(m)], y_ref.at[me_rows, c], l_send.at[m], l_recv.at[m], peer)

    def g_copies(m):
        bands = [pl.ds(pl.multiple_of(tp_l * q, h), h), pl.ds(pl.multiple_of(tp_r * q + h, h), h)]
        return [remote(y_ref.at[bands[i], ycols(m, e)], y_ref.at[bands[i], ycols(m, e)], g_send.at[i, e, m],
                       g_recv.at[i, e, m], side[i]) for i in range(2) for e in range(2)]

    def spread(t_ref, c):
        for g in range(2):
            r = g * rows
            k_me[g, :, c] = t_ref[pl.ds(pl.multiple_of(r + tp * q, q), q), :]
            k_n[0, g, :, c] = t_ref[pl.ds(pl.multiple_of(r + tp_r * q, h), h), :]
            k_n[1, g, :, c] = t_ref[pl.ds(pl.multiple_of(r + tp_l * q + h, h), h), :]
            a_out[0, 0, g, :, c] = t_ref[pl.ds(pl.multiple_of(r + tp_f * q, h), h), :].astype(a_out.dtype)
            a_out[1, 0, g, :, c] = t_ref[pl.ds(pl.multiple_of(r + tp_f * q + h, h), h), :].astype(a_out.dtype)
            a_out[0, 1, g, :, c] = t_ref[pl.ds(pl.multiple_of(r + tp_r * q + h, h), h), :].astype(a_out.dtype)
            a_out[1, 1, g, :, c] = t_ref[pl.ds(pl.multiple_of(r + tp_l * q, h), h), :].astype(a_out.dtype)

    def down(scratch):
        for j in range(nb):
            hid_copy(j).wait_recv()

        @pl.loop(0, nc + LG)
        def _(it):
            @pl.when(it < nc)
            def _():
                m = it
                down_copy(m).wait()
                scratch[...] = jnp.dot(hid[...], wd[lax.rem(m, ND)], preferred_element_type=F32)
                spread(scratch, chunk(m))
                for cp in a_copies(m):
                    cp.start()

                @pl.when(m + ND < nc)
                def _():
                    down_copy(m + ND).start()

            @pl.when((it >= LB) & (it < nc + LB))
            def _():
                m = it - LB
                c = chunk(m)
                for cp in a_copies(m):
                    cp.wait_recv()
                for i in range(2):
                    for g in range(2):
                        b_out[i, g, :, c] = (k_n[i, g, :, c] + a_in[i, 0, g, :, c].astype(F32)).astype(b_out.dtype)
                for cp in b_copies(m):
                    cp.start()

            @pl.when((it >= LF) & (it < nc + LF))
            def _():
                m = it - LF
                c = chunk(m)
                for cp in b_copies(m):
                    cp.wait_recv()

                def total(g):
                    top = k_me[g, pl.ds(0, h), c] + b_in[0, g, :, c].astype(F32) + a_in[1, 1, g, :, c].astype(F32)
                    bot = k_me[g, pl.ds(h, h), c] + a_in[0, 1, g, :, c].astype(F32) + b_in[1, g, :, c].astype(F32)
                    return top.astype(y_ref.dtype), bot.astype(y_ref.dtype)

                top, bot = total(core)
                r = pl.multiple_of(tp * q, q)
                y_ref[pl.ds(r, h), ycols(m, core)] = top
                y_ref[pl.ds(pl.multiple_of(r + h, h), h), ycols(m, core)] = bot
                top, bot = total(other)
                f_out[pl.ds(0, h), c] = top
                f_out[pl.ds(h, h), c] = bot
                for cp in f_copies(m):
                    cp.start()
                l_copy(m).start()

            @pl.when(it >= LG)
            def _():
                m = it - LG
                for cp in f_waits(m):
                    cp.wait_recv()
                for cp in g_copies(m):
                    cp.start()

    pl.run_scoped(down, pltpu.VMEM((2 * rows, CB), F32))

    peer_x.wait_send()

    @pl.loop(0, nb)
    def _(j):
        hid_copy(j).wait_send()

    @pl.loop(0, nc)
    def _(m):
        for cp in a_copies(m) + b_copies(m) + f_copies(m):
            cp.wait_send()
        l_copy(m).wait()
        for cp in g_copies(m):
            cp.wait()


def solution(mesh):
    def step(x, w_gate, w_up, w_down):
        rows, d = x.shape
        ff = w_gate.shape[1] // 2
        dh = d // 2
        q = rows // mesh.shape["tp"]
        h = q // 2
        nb = ff // HB
        nc = dh // CB
        bf = x.dtype
        vm = pltpu.VMEM
        dma = pltpu.SemaphoreType.DMA
        hbm = pl.BlockSpec(memory_space=pl.ANY)
        return pl.pallas_call(
            kernel,
            out_shape=pltpu.VMEM((rows, d), bf),
            in_specs=[hbm] * 4,
            out_specs=pl.BlockSpec(memory_space=pltpu.VMEM),
            scratch_shapes=[
                vm((2 * rows, d), bf),
                vm((NS, d, HB), bf),
                vm((NS, d, HB), bf),
                vm((ND, 2 * ff, CB), bf),
                vm((2 * rows, 2 * ff), bf),
                vm((2, q, dh), F32),
                vm((2, 2, h, dh), F32),
                vm((2, 2, 2, h, dh), bf),
                vm((2, 2, 2, h, dh), bf),
                vm((2, 2, h, dh), bf),
                vm((2, 2, h, dh), bf),
                vm((q, dh), bf),
                dma, dma, dma, dma((NS,)), dma((NS,)), dma((ND,)), dma((nb,)), dma((nb,)),
                dma((2, nc)), dma((2, nc)), dma((2, nc)), dma((2, nc)),
                dma((2, 2, nc)), dma((2, 2, nc)), dma((nc,)), dma((nc,)), dma((2, 2, nc)), dma((2, 2, nc)),
            ],
            compiler_params=pltpu.CompilerParams(
                collective_id=0, has_side_effects=True, vmem_limit_bytes=65000000),
        )(x, w_gate, w_up, w_down)

    return jax.shard_map(
        step,
        mesh=mesh,
        in_specs=(P("dp", None), P(None, "tp"), P(None, "tp"), P("tp", None)),
        out_specs=P("dp", None),
        check_vma=False,
    )
```

time: 146 us -> 67.6 us (0.46)
  matrix products: 78.6 us -> 0 us
  Pallas kernels: 0 us -> 66.1 us
  waiting for transfers between devices: 49.1 us -> 0 us
  between operations: 13.4 us -> 0.01 us
  local copies, waits for them, and re-layouts: 4.34 us -> 1.23 us
    dot_general x3 -> x0, matrix products: 78.6 us -> none  [the longest x1 26.3 us: step(): gate = jnp.dot(x, w_gate, preferred_element_type=jnp.float32)]
    pallas_call x0 -> x1, Pallas kernels: none -> 66.1 us  [step(): pl.pallas_call(kernel, out_shape=pltpu.VMEM((rows, d), bf), in_specs=[hbm...]
    psum x1 -> x0, waiting for transfers between devices: 49.1 us -> none  [step(): return lax.psum(term, 'tp')]
    unnamed x3 -> x1, local copies, waits for them, and re-layouts: 4.34 us -> 1.23 us
  transfers between devices with their start and end apart: 1 -> 0, of which waited for: 1 -> 0; matrix products, arithmetic and copies ran while one was open for 0% -> 0% of each run, Pallas kernels for 0% -> 0%
where the time goes in v2:
time: 67.6 us; the launch traced here: 67.4 us
  Pallas kernels  66.1 us (98%)
  local copies, waits for them, and re-layouts  1.23 us (2%)
    pallas_call x1, Pallas kernels, step(): pl.pallas_call(kernel, out_shape=pltpu.VMEM((rows, d), bf), in_specs=[hbm...  66.1 us

profile of v2, /device:TPU:112, one launch (start us, length us, event | category | flops | bytes accessed | tf_op | source)
XLA Modules:
  0.0 67.4 jit_solution(1945020970377851948)
XLA Ops:
  0.0 66.1 %shard_map.46 = bf16[128,7168]{1,0:T(8,128)(2,1)S(1)} custom-call(bf16[128,7168]{1,0:T(8,128)(2,1)} %x_ref.1, bf16[7168,5120]{1,0:T(8,128)(2,1)} %wg_ref.1, bf16[7168,5120]{1,0:T(8,128)(2,1)} %wu_ref.1, bf16[5120,7168]{1,0:T(8,128)(2,1)} %wd_ref.1), custom_call_target="tpu_custom_call" | custom-call | tf_op jit(solution)/shard_map/pallas_call | solution.py:276
  66.2 1.2 %copy.6 = bf16[128,7168]{1,0:T(8,128)(2,1)} copy(bf16[128,7168]{1,0:T(8,128)(2,1)S(1)} %shard_map.46) | data formatting | bytes 3670016

commit v3 on v0

v3 whole, which is shorter than its diff:
```python
import jax
import jax.numpy as jnp
from jax import lax
from jax.experimental import pallas as pl
from jax.experimental.pallas import tpu as pltpu
from jax.sharding import PartitionSpec as P

MESH = pl.DeviceIdType.MESH
F32 = jnp.float32
HB = 256
KC = 2
NS = 4
CB = 512
ND = 3
LB = 3
LF = 7
LG = 11


def kernel(
    x_ref, wg_ref, wu_ref, wd_ref, y_ref,
    xbuf, wg, wu, wd, hid, k_me, k_n, a_out, a_in, b_out, b_in, f_out, part,
    x_sem, xs_sem, xr_sem, g_sem, u_sem, d_sem, h_send, h_recv,
    a_send, a_recv, b_send, b_recv, f_send, f_recv, l_send, l_recv, g_send, g_recv,
):
    rows, d = x_ref.shape
    ff = wg_ref.shape[1] // 2
    dh = d // 2
    n = 4
    nb = ff // HB
    nc = dh // CB
    q = rows // n
    h = q // 2
    kd = d // KC
    dp, tp = lax.axis_index("dp"), lax.axis_index("tp")
    core = lax.rem(dp, 2)
    other = 1 - core
    dp_peer = dp + 1 - 2 * core
    tp_r, tp_l = lax.rem(tp + 1, n), lax.rem(tp + n - 1, n)
    peer = {"dp": dp_peer, "tp": tp}
    side = [{"dp": dp, "tp": tp_r}, {"dp": dp, "tp": tp_l}]
    side_peer = [{"dp": dp_peer, "tp": tp_r}, {"dp": dp_peer, "tp": tp_l}]
    base = core * ff
    cbase = core * dh
    own_r = pl.multiple_of(core * rows, rows)
    peer_r = pl.multiple_of(other * rows, rows)

    def remote(src, dst, send, recv, to):
        return pltpu.make_async_remote_copy(
            src_ref=src, dst_ref=dst, send_sem=send, recv_sem=recv, device_id=to, device_id_type=MESH)

    def hcols(j):
        return pl.ds(pl.multiple_of(base + j * HB, HB), HB)

    def gate_up_copies(j, kc):
        s = lax.rem(j, NS)
        k = pl.ds(kc * kd, kd)
        return [pltpu.make_async_copy(wg_ref.at[k, hcols(j)], wg.at[s, k], g_sem.at[s, kc]),
                pltpu.make_async_copy(wu_ref.at[k, hcols(j)], wu.at[s, k], u_sem.at[s, kc])]

    def start_block(j):
        for kc in range(KC):
            for cp in gate_up_copies(j, kc):
                cp.start()

    def k_half(e):
        return pl.ds(pl.multiple_of((core if e == 0 else other) * ff, HB), ff)

    def down_copies(m):
        s = lax.rem(m, ND)
        c = pl.ds(pl.multiple_of(cbase + m * CB, CB), CB)
        return [pltpu.make_async_copy(wd_ref.at[k_half(e), c], wd.at[s, k_half(e)], d_sem.at[s, e])
                for e in range(2)]

    def hid_copy(j):
        b = core * nb + j
        return remote(hid.at[b], hid.at[b], h_send.at[j], h_recv.at[j], peer)

    own_x = [pltpu.make_async_copy(
        x_ref.at[pl.ds(pl.multiple_of(lax.rem(tp + i, n) * q, q), q)],
        xbuf.at[pl.ds(pl.multiple_of(own_r + i * q, q), q)], x_sem.at[i]) for i in range(n)]
    for cp in own_x:
        cp.start()
    start_block(0)
    barrier = pltpu.get_barrier_semaphore()
    for to in [peer] + side + side_peer:
        pl.semaphore_signal(barrier, inc=1, device_id=to, device_id_type=MESH)
    for j in range(1, NS):
        start_block(j)
    for cp in own_x:
        cp.wait()
    pl.semaphore_wait(barrier, 5)
    peer_x = remote(xbuf.at[pl.ds(own_r, rows)], xbuf.at[pl.ds(own_r, rows)], xs_sem, xr_sem, peer)
    peer_x.start()

    def chunk(m):
        return pl.ds(pl.multiple_of(m * CB, CB), CB)

    def ycols(c, half):
        return pl.ds(pl.multiple_of(half * dh + c * CB, CB), CB)

    def a_copies(m):
        return [remote(a_out.at[i, m], a_in.at[i, m], a_send.at[i, m], a_recv.at[i, m], side[i]) for i in range(2)]

    def b_copies(m):
        return [remote(b_out.at[i, m], b_in.at[i, m], b_send.at[i, m], b_recv.at[i, m], side[i]) for i in range(2)]

    me_rows = pl.ds(pl.multiple_of(tp * q, q), q)

    def f_copies(m):
        c = ycols(m, core)
        out = []
        for i in range(2):
            out.append(remote(y_ref.at[me_rows, c], y_ref.at[me_rows, c], f_send.at[i, 0, m],
                              f_recv.at[i, core, m], side[i]))
            out.append(remote(f_out.at[m], y_ref.at[me_rows, c], f_send.at[i, 1, m],
                              f_recv.at[i, core, m], side_peer[i]))
        return out

    def f_waits(m):
        return [remote(y_ref.at[me_rows, ycols(m, e)], y_ref.at[me_rows, ycols(m, e)], f_send.at[i, 0, m],
                       f_recv.at[i, e, m], side[i]) for i in range(2) for e in range(2)]

    def l_copy(m):
        return remote(f_out.at[m], y_ref.at[me_rows, ycols(m, core)], l_send.at[m], l_recv.at[m], peer)

    def g_copies(m):
        bands = [pl.ds(pl.multiple_of(tp_l * q, h), h), pl.ds(pl.multiple_of(tp_r * q + h, h), h)]
        return [remote(y_ref.at[bands[i], ycols(m, e)], y_ref.at[bands[i], ycols(m, e)], g_send.at[i, e, m],
                       g_recv.at[i, e, m], side[i]) for i in range(2) for e in range(2)]

    def gate_up(j, r0, nr):
        s = lax.rem(j, NS)
        xs = xbuf[pl.ds(r0, nr), :]
        g = jnp.dot(xs, wg[s], preferred_element_type=F32)
        u = jnp.dot(xs, wu[s], preferred_element_type=F32)
        hid[core * nb + j, pl.ds(r0, nr)] = (jax.nn.silu(g) * u).astype(hid.dtype)

    def wait_block(j, kc):
        for cp in gate_up_copies(j, kc):
            cp.wait()

    def refill(j):
        @pl.when(j + NS < nb)
        def _():
            start_block(j + NS)

        @pl.when(j + NS == nb)
        def _():
            for m in range(ND):
                for cp in down_copies(m):
                    cp.start()

    for kc in range(KC):
        wait_block(0, kc)
    gate_up(0, own_r, rows)
    peer_x.wait_recv()
    gate_up(0, peer_r, rows)
    refill(0)

    @pl.loop(1, nb - 1)
    def _(j):
        for kc in range(KC):
            wait_block(j, kc)
        hid_copy(j - 1).start()
        gate_up(j, 0, 2 * rows)
        refill(j)

    last = nb - 1
    sl = last % NS
    for kc in range(KC):
        wait_block(last, kc)
        if kc == 0:
            hid_copy(last - 1).start()
        k = pl.ds(kc * kd, kd)
        g = jnp.dot(xbuf[:, k], wg[sl, k, :], preferred_element_type=F32)
        u = jnp.dot(xbuf[:, k], wu[sl, k, :], preferred_element_type=F32)
        if kc > 0:
            g += part[:, pl.ds(0, HB)]
            u += part[:, pl.ds(HB, HB)]
        if kc < KC - 1:
            part[:, pl.ds(0, HB)] = g
            part[:, pl.ds(HB, HB)] = u
    hid[core * nb + last] = (jax.nn.silu(g) * u).astype(hid.dtype)
    hid_copy(last).start()

    def spread(m, t):
        tb = t.astype(a_out.dtype)
        for g in range(2):
            r = g * rows
            k_me[m, g] = t[r:r + q]
            k_n[m, 0, g] = t[r + q:r + q + h]
            k_n[m, 1, g] = t[r + 3 * q + h:r + 4 * q]
            a_out[0, m, pl.ds(g * h, h)] = tb[r + 2 * q:r + 2 * q + h]
            a_out[1, m, pl.ds(g * h, h)] = tb[r + 2 * q + h:r + 3 * q]
            a_out[0, m, pl.ds((2 + g) * h, h)] = tb[r + q + h:r + 2 * q]
            a_out[1, m, pl.ds((2 + g) * h, h)] = tb[r + 3 * q:r + 3 * q + h]

    def first_hop(m):
        for cp in a_copies(m):
            cp.start()

    def second_hop(m):
        for cp in a_copies(m):
            cp.wait_recv()
        for i in range(2):
            for g in range(2):
                r = pl.ds(g * h, h)
                b_out[i, m, r] = (k_n[m, i, g] + a_in[i, m, r].astype(F32)).astype(b_out.dtype)
        for cp in b_copies(m):
            cp.start()

    def finish(m):
        for cp in b_copies(m):
            cp.wait_recv()

        def total(g):
            g0 = pl.ds(pl.multiple_of(g * h, h), h)
            g1 = pl.ds(pl.multiple_of((2 + g) * h, h), h)
            top = k_me[m, g, pl.ds(0, h)] + b_in[0, m, g0].astype(F32) + a_in[1, m, g1].astype(F32)
            bot = k_me[m, g, pl.ds(h, h)] + a_in[0, m, g1].astype(F32) + b_in[1, m, g0].astype(F32)
            return top.astype(y_ref.dtype), bot.astype(y_ref.dtype)

        top, bot = total(core)
        r = pl.multiple_of(tp * q, q)
        y_ref[pl.ds(r, h), ycols(m, core)] = top
        y_ref[pl.ds(pl.multiple_of(r + h, h), h), ycols(m, core)] = bot
        top, bot = total(other)
        f_out[m, pl.ds(0, h)] = top
        f_out[m, pl.ds(h, h)] = bot
        for cp in f_copies(m):
            cp.start()
        l_copy(m).start()

    def forward(m):
        for cp in f_waits(m):
            cp.wait_recv()
        for cp in g_copies(m):
            cp.start()

    def refill_down(m):
        @pl.when(m + ND < nc)
        def _():
            for cp in down_copies(m + ND):
                cp.start()

    def hidden(first, count):
        return jnp.concatenate([hid[first + b] for b in range(count)], axis=1)

    def down_part(e, b0, count):
        who = core if e == 0 else other
        k = pl.ds(pl.multiple_of(who * ff + b0 * HB, HB), count * HB)
        return jnp.dot(hidden(who * nb + b0, count), wd[0, k], preferred_element_type=F32)

    down_copies(0)[0].wait()
    part[...] = down_part(0, 0, nb)
    for j in range(nb - 1):
        hid_copy(j).wait_recv()
    down_copies(0)[1].wait()
    part[...] += down_part(1, 0, nb - 1)
    hid_copy(nb - 1).wait_recv()
    spread(0, part[...] + down_part(1, nb - 1, 1))
    first_hop(0)
    refill_down(0)

    @pl.loop(1, nc + LG)
    def _(it):
        @pl.when(it < nc)
        def _():
            for cp in down_copies(it):
                cp.wait()
            spread(it, jnp.dot(hidden(0, 2 * nb), wd[lax.rem(it, ND)], preferred_element_type=F32))
            first_hop(it)
            refill_down(it)

        @pl.when((it >= LB) & (it < nc + LB))
        def _():
            second_hop(it - LB)

        @pl.when((it >= LF) & (it < nc + LF))
        def _():
            finish(it - LF)

        @pl.when(it >= LG)
        def _():
            forward(it - LG)

    peer_x.wait_send()

    @pl.loop(0, nb)
    def _(j):
        hid_copy(j).wait_send()

    @pl.loop(0, nc)
    def _(m):
        for cp in a_copies(m) + b_copies(m) + f_copies(m):
            cp.wait_send()
        l_copy(m).wait()
        for cp in g_copies(m):
            cp.wait()


def solution(mesh):
    def step(x, w_gate, w_up, w_down):
        rows, d = x.shape
        ff = w_gate.shape[1] // 2
        n = mesh.shape["tp"]
        q = rows // n
        h = q // 2
        nb = ff // HB
        nc = d // 2 // CB
        bf = x.dtype
        vm = pltpu.VMEM
        dma = pltpu.SemaphoreType.DMA
        hbm = pl.BlockSpec(memory_space=pl.ANY)
        return pl.pallas_call(
            kernel,
            out_shape=pltpu.VMEM((rows, d), bf),
            in_specs=[hbm] * 4,
            out_specs=pl.BlockSpec(memory_space=pltpu.VMEM),
            scratch_shapes=[
                vm((2 * rows, d), bf),
                vm((NS, d, HB), bf),
                vm((NS, d, HB), bf),
                vm((ND, 2 * ff, CB), bf),
                vm((2 * nb, 2 * rows, HB), bf),
                vm((nc, 2, q, CB), F32),
                vm((nc, 2, 2, h, CB), F32),
                vm((2, nc, 2 * q, CB), bf),
                vm((2, nc, 2 * q, CB), bf),
                vm((2, nc, q, CB), bf),
                vm((2, nc, q, CB), bf),
                vm((nc, q, CB), bf),
                vm((2 * rows, 2 * HB), F32),
                dma((n,)), dma, dma, dma((NS, KC)), dma((NS, KC)), dma((ND, 2)), dma((nb,)), dma((nb,)),
                dma((2, nc)), dma((2, nc)), dma((2, nc)), dma((2, nc)),
                dma((2, 2, nc)), dma((2, 2, nc)), dma((nc,)), dma((nc,)), dma((2, 2, nc)), dma((2, 2, nc)),
            ],
            compiler_params=pltpu.CompilerParams(
                collective_id=0, has_side_effects=True, vmem_limit_bytes=65000000),
        )(x, w_gate, w_up, w_down)

    return jax.shard_map(
        step,
        mesh=mesh,
        in_specs=(P("dp", None), P(None, "tp"), P(None, "tp"), P("tp", None)),
        out_specs=P("dp", None),
        check_vma=False,
    )
```

time: 146 us -> 66.1 us (0.45)
  matrix products: 78.6 us -> 0 us
  Pallas kernels: 0 us -> 64.8 us
  waiting for transfers between devices: 49.1 us -> 0 us
  between operations: 13.4 us -> 0.01 us
  local copies, waits for them, and re-layouts: 4.34 us -> 1.23 us
    dot_general x3 -> x0, matrix products: 78.6 us -> none  [the longest x1 26.3 us: step(): gate = jnp.dot(x, w_gate, preferred_element_type=jnp.float32)]
    pallas_call x0 -> x1, Pallas kernels: none -> 64.8 us  [step(): pl.pallas_call(kernel, out_shape=pltpu.VMEM((rows, d), bf), in_specs=[hbm...]
    psum x1 -> x0, waiting for transfers between devices: 49.1 us -> none  [step(): return lax.psum(term, 'tp')]
    unnamed x3 -> x1, local copies, waits for them, and re-layouts: 4.34 us -> 1.23 us
  transfers between devices with their start and end apart: 1 -> 0, of which waited for: 1 -> 0; matrix products, arithmetic and copies ran while one was open for 0% -> 0% of each run, Pallas kernels for 0% -> 0%
where the time goes in v3:
time: 66.1 us
  Pallas kernels  64.8 us (98%)
  local copies, waits for them, and re-layouts  1.23 us (2%)
    pallas_call x1, Pallas kernels, step(): pl.pallas_call(kernel, out_shape=pltpu.VMEM((rows, d), bf), in_specs=[hbm...  64.8 us

profile of v3, /device:TPU:112, one launch (start us, length us, event | category | flops | bytes accessed | tf_op | source)
XLA Modules:
  0.0 66.1 jit_solution(10089251729488861441)
XLA Ops:
  0.0 64.8 %shard_map.46 = bf16[128,7168]{1,0:T(8,128)(2,1)S(1)} custom-call(bf16[128,7168]{1,0:T(8,128)(2,1)} %x_ref.1, bf16[7168,5120]{1,0:T(8,128)(2,1)} %wg_ref.1, bf16[7168,5120]{1,0:T(8,128)(2,1)} %wu_ref.1, bf16[5120,7168]{1,0:T(8,128)(2,1)} %wd_ref.1), custom_call_target="tpu_custom_call" | custom-call | tf_op jit(solution)/shard_map/pallas_call | solution.py:316
  64.8 1.2 %copy.6 = bf16[128,7168]{1,0:T(8,128)(2,1)} copy(bf16[128,7168]{1,0:T(8,128)(2,1)S(1)} %shard_map.46) | data formatting | bytes 3670016

commit v4 on v3

--- a/solution.py
+++ b/solution.py
@@ -1,3 +1,5 @@
+import functools
+
 import jax
 import jax.numpy as jnp
 from jax import lax
@@ -9,6 +11,7 @@
 F32 = jnp.float32
 HB = 256
 KC = 2
+OWN = 2
 NS = 4
 CB = 512
 ND = 3
@@ -18,7 +21,7 @@
 
 
 def kernel(
-    x_ref, wg_ref, wu_ref, wd_ref, y_ref,
+    n, x_ref, wg_ref, wu_ref, wd_ref, y_ref,
     xbuf, wg, wu, wd, hid, k_me, k_n, a_out, a_in, b_out, b_in, f_out, part,
     x_sem, xs_sem, xr_sem, g_sem, u_sem, d_sem, h_send, h_recv,
     a_send, a_recv, b_send, b_recv, f_send, f_recv, l_send, l_recv, g_send, g_recv,
@@ -26,7 +29,6 @@
     rows, d = x_ref.shape
     ff = wg_ref.shape[1] // 2
     dh = d // 2
-    n = 4
     nb = ff // HB
     nc = dh // CB
     q = rows // n
@@ -151,14 +153,23 @@
                 for cp in down_copies(m):
                     cp.start()
 
-    for kc in range(KC):
-        wait_block(0, kc)
-    gate_up(0, own_r, rows)
+    @pl.loop(0, OWN)
+    def _(j):
+        for kc in range(KC):
+            wait_block(j, kc)
+        gate_up(j, own_r, rows)
+
     peer_x.wait_recv()
-    gate_up(0, peer_r, rows)
-    refill(0)
-
-    @pl.loop(1, nb - 1)
+
+    @pl.loop(0, OWN)
+    def _(j):
+        gate_up(j, peer_r, rows)
+        refill(j)
+
+    for j in range(OWN - 1):
+        hid_copy(j).start()
+
+    @pl.loop(OWN, nb - 1)
     def _(j):
         for kc in range(KC):
             wait_block(j, kc)
@@ -314,7 +325,7 @@
         dma = pltpu.SemaphoreType.DMA
         hbm = pl.BlockSpec(memory_space=pl.ANY)
         return pl.pallas_call(
-            kernel,
+            functools.partial(kernel, n),
             out_shape=pltpu.VMEM((rows, d), bf),
             in_specs=[hbm] * 4,
             out_specs=pl.BlockSpec(memory_space=pltpu.VMEM),

time: 66.1 us -> 66.1 us (level)
  no operation moved by 1% of the time
where the time goes in v4:
time: 66.1 us; the launch traced here: 66 us
  Pallas kernels  64.8 us (98%)
  local copies, waits for them, and re-layouts  1.23 us (2%)
    pallas_call x1, Pallas kernels, step(): pl.pallas_call(functools.partial(kernel, n), out_shape=pltpu.VMEM((rows,...  64.8 us

profile of v4, /device:TPU:112, one launch (start us, length us, event | category | flops | bytes accessed | tf_op | source)
XLA Modules:
  0.0 66.0 jit_solution(5788623877178014239)
XLA Ops:
  0.0 64.8 %shard_map.46 = bf16[128,7168]{1,0:T(8,128)(2,1)S(1)} custom-call(bf16[128,7168]{1,0:T(8,128)(2,1)} %x_ref.1, bf16[7168,5120]{1,0:T(8,128)(2,1)} %wg_ref.1, bf16[7168,5120]{1,0:T(8,128)(2,1)} %wu_ref.1, bf16[5120,7168]{1,0:T(8,128)(2,1)} %wd_ref.1), custom_call_target="tpu_custom_call" | custom-call | tf_op jit(solution)/shard_map/pallas_call | solution.py:327
  64.8 1.2 %copy.6 = bf16[128,7168]{1,0:T(8,128)(2,1)} copy(bf16[128,7168]{1,0:T(8,128)(2,1)S(1)} %shard_map.46) | data formatting | bytes 3670016
